TPU v7x, 32 devices: a whole 2x2x4 slice. The times are simulated.
32 devices in a mesh: row: 16 (over z, y, core), col: 2 (over x).
Axes of the slice: x: 2, y: 2, z: 4, core: 2. Of those that a mesh axis runs over, the one named last changes fastest.
Arguments:
- vectors: float32 [1024, 32768], P(('row', 'col')), may hold values from -6 to 6
- reflectors: float32 [6, 128, 32768], P(None, 'col', 'row')
- factors: float32 [6, 128, 128], replicated, as said below
Outputs:
- transformed: float32 [1024, 32768], P('col', 'row')
Inputs may be any that keep to these rules, and one draw needn't show every extreme that they name: factors[k] is upper triangular, and its inverse equals the strict upper part of reflectors[k] reflectors[k]^T plus half of that product's diagonal, so each panel is orthogonal.
All inputs are finite; a program needn't handle non-finite values.
Results may differ from a plain program's by a relative error of at most 0.0001.
Values sent between devices are 32-bit elements; how exact they have to be, the bound alone decides.
A program may use at most 128 MiB of HBM per device.

v0:
```python
import functools

import jax
import jax.numpy as jnp
from jax import lax
from jax.experimental import pallas as pl
from jax.experimental.pallas import tpu as pltpu
from jax.sharding import PartitionSpec as P

MESH = pl.DeviceIdType.MESH
HIGH = lax.Precision.HIGH


def nt(left, right, precision):
    return lax.dot_general(
        left,
        right,
        (((1,), (1,)), ((), ())),
        precision=precision,
        preferred_element_type=jnp.float32,
    )


def split(value):
    top = value.astype(jnp.bfloat16)
    return top, (value - top.astype(jnp.float32)).astype(jnp.bfloat16)


def plain_nt(left, right):
    return lax.dot_general(
        left, right, (((1,), (1,)), ((), ())), preferred_element_type=jnp.float32
    )


def strides_of(rows):
    found = []
    stride = 1
    while stride < rows:
        found.append(stride)
        stride *= 2
    return found


def orders_of(rows):
    base = strides_of(rows)
    return [base, base[:1] + base[2:] + base[1:2]]


class Reduce:
    def __init__(self, row, row_count, source, landing, out, sems):
        self.row = row
        self.source = source
        self.landing = landing
        self.out = out
        self.sems = sems
        total = source.shape[0]
        self.orders = orders_of(row_count)
        self.part = total // len(self.orders)
        self.previous = [source.at[pl.ds(i * self.part, self.part)] for i in range(2)]
        self.offset = [i * self.part for i in range(2)]
        self.count = len(self.orders[0])
        self.pending = None

    def bit(self, stride):
        return lax.rem(self.row // stride, 2)

    def partner(self, stride):
        return self.row + stride * (1 - 2 * self.bit(stride))

    def copy(self, source, target, number, stride):
        return pltpu.make_async_remote_copy(
            src_ref=source,
            dst_ref=target,
            send_sem=self.sems.at[0, number],
            recv_sem=self.sems.at[1, number],
            device_id={"row": self.partner(stride)},
            device_id_type=MESH,
        )

    def halve_start(self, stage):
        self.pending = []
        half = self.part >> (stage + 1)
        start = self.part - (self.part >> stage)
        for i in range(2):
            stride = self.orders[i][stage]
            bit = self.bit(stride)
            away = pl.ds(pl.multiple_of((1 - bit) * half, 8), half)
            here = self.landing.at[i, pl.ds(start, half)]
            item = self.copy(self.previous[i].at[away], here, stage * 2 + i, stride)
            item.start()
            self.pending.append((item, here, bit, half))

    def halve_end(self):
        for i in range(2):
            item, here, bit, half = self.pending[i]
            item.wait()
            keep = pl.ds(pl.multiple_of(bit * half, 8), half)
            here[...] = here[...] + self.previous[i][keep, :]
            self.previous[i] = here
            self.offset[i] = self.offset[i] + bit * half

    def place(self, i, value):
        size = value.shape[0]
        self.out[pl.ds(pl.multiple_of(self.offset[i], 8), size), :] = value

    def double_start(self, stage):
        self.pending = []
        size = self.part >> (self.count - stage)
        for i in range(2):
            stride = self.orders[i][self.count - 1 - stage]
            where = self.out.at[pl.ds(pl.multiple_of(self.offset[i], 8), size)]
            item = self.copy(where, where, (self.count + stage) * 2 + i, stride)
            item.start()
            self.pending.append((item, self.bit(stride) * size))

    def double_end(self):
        for i in range(2):
            item, back = self.pending[i]
            item.wait()
            self.offset[i] = self.offset[i] - back


def kernel(
    row_count, col_count, vectors, reflectors, factors, current, panels, update,
    stage, held, tops, lows, here, here_top, here_low, projection, solved_rows,
    landing, partial, gram, gram_landing,
    row_sems, far_sems, gather_sems, local_sems, out_sems, gram_sems, first_sems, second_sems,
):
    row = lax.axis_index("row")
    col = lax.axis_index("col")
    local = vectors.shape[0]
    length = current.shape[1]
    count, part, _ = reflectors.shape
    width = part * col_count
    group = row_count // col_count
    half_slots = row_count // 2
    half_rows = half_slots * local

    barrier = pltpu.get_barrier_semaphore()
    for step in range(1, row_count):
        pl.semaphore_signal(
            barrier, inc=1, device_id={"row": lax.rem(row + step, row_count)}, device_id_type=MESH
        )
    for step in range(1, col_count):
        pl.semaphore_signal(
            barrier, inc=1, device_id={"col": lax.rem(col + step, col_count)}, device_id_type=MESH
        )
    pl.semaphore_wait(barrier, row_count + col_count - 2)

    def slot_rows(slot):
        return pl.ds(pl.multiple_of(slot * local, 8), local)

    gathers = []
    for step in range(1, col_count):
        for panel in range(count):
            number = (step - 1) * count + panel
            item = pltpu.make_async_remote_copy(
                src_ref=reflectors.at[panel],
                dst_ref=held.at[pl.ds(pl.multiple_of(panel * width + col * part, 8), part)],
                send_sem=gather_sems.at[0, number],
                recv_sem=gather_sems.at[1, number],
                device_id={"col": lax.rem(col + step, col_count)},
                device_id_type=MESH,
            )
            item.start()
            gathers.append(item)

    def onward(source_row):
        block = source_row * col_count + col
        target = block // row_count
        slot = lax.rem(block, row_count)
        place = lax.rem(slot - target + col_count, col_count) * group + slot // col_count
        return target, place

    middle = row_count // 2
    ranked = sorted(range(1, row_count), key=lambda step: (abs(step - middle), step))
    steps = []
    while ranked:
        steps.append(ranked.pop(0))
        if ranked:
            steps.append(ranked.pop())
    my_target, my_place = onward(row)
    sends = {}
    for step in steps:
        other = lax.rem(row + step, row_count)
        source = vectors.at[:, pl.ds(pl.multiple_of(other * length, 128), length)]

        def sending(target, source=source, step=step, other=other):
            return pltpu.make_async_remote_copy(
                src_ref=source,
                dst_ref=target,
                send_sem=row_sems.at[0, step],
                recv_sem=row_sems.at[1, step],
                device_id={"row": other},
                device_id_type=MESH,
            )

        @pl.when(my_target == col)
        def _():
            sending(here.at[slot_rows(my_place)]).start()

        @pl.when(my_target != col)
        def _():
            sending(stage.at[row]).start()

        sends[step] = sending(stage.at[row])

    own = pltpu.make_async_copy(
        vectors.at[:, pl.ds(pl.multiple_of(row * length, 128), length)], stage.at[row], local_sems.at[0]
    )
    own.start()
    own_panels = []
    for panel in range(count):
        item = pltpu.make_async_copy(
            reflectors.at[panel],
            held.at[pl.ds(pl.multiple_of(panel * width + col * part, 8), part)],
            local_sems.at[1 + panel],
        )
        item.start()
        own_panels.append(item)

    def far_copy(source_row):
        target, place = onward(source_row)
        return target, pltpu.make_async_remote_copy(
            src_ref=stage.at[source_row],
            dst_ref=here.at[slot_rows(place)],
            send_sem=far_sems.at[0, place],
            recv_sem=far_sems.at[1, place],
            device_id={"col": target},
            device_id_type=MESH,
        )

    own.wait()
    own_target, own_far = far_copy(row)
    own_here = pltpu.make_async_copy(stage.at[row], here.at[slot_rows(my_place)], local_sems.at[0])

    @pl.when(own_target == col)
    def _():
        own_here.start()
        own_here.wait()

    @pl.when(own_target != col)
    def _():
        own_far.start()

    def arrive(step):
        target, far = far_copy(lax.rem(row - step + row_count, row_count))
        sends[step].wait_recv()

        @pl.when(target != col)
        def _():
            far.start()

    early = len(steps) // 5
    for step in steps[:early]:
        arrive(step)
    for item in own_panels:
        item.wait()
    for item in gathers:
        item.wait()
    keep_panels = pltpu.make_async_copy(held, panels, local_sems.at[0])
    keep_panels.start()

    def split_rows(i, carry):
        rows = pl.ds(pl.multiple_of(i * 32, 32), 32)
        top, low = split(held[rows, :])
        tops[rows, :] = top
        lows[rows, :] = low
        return carry

    lax.fori_loop(0, count * width // 32, split_rows, 0)
    base = 0
    starts = []
    for panel in range(count):
        starts.append(base)
        right = pl.ds(panel * width, width)

        def block(i, carry, right=right, base=base, panel=panel):
            left = pl.ds(pl.multiple_of((panel + 1 + i) * width, 128), width)
            value = plain_nt(tops[left, :], tops[right, :])
            value = value + plain_nt(tops[left, :], lows[right, :])
            value = value + plain_nt(lows[left, :], tops[right, :])
            partial[pl.ds(pl.multiple_of(base + i * width, 128), width), :] = value
            return carry

        if panel < count - 1:
            lax.fori_loop(0, count - 1 - panel, block, 0)
        base += (count - 1 - panel) * width
    partial[pl.ds(base, partial.shape[0] - base), :] = jnp.zeros(
        (partial.shape[0] - base, width), jnp.float32
    )

    def put_out(source, target, place, which):
        slot = (place % group) * col_count + lax.rem(col + place // group, col_count)
        item = pltpu.make_async_copy(
            source.at[slot_rows(place)], target.at[slot_rows(slot)], out_sems.at[which, place]
        )
        item.start()
        return item

    outs = []
    tile = 2 * width if count % 2 == 0 else width

    def project(chunk):
        for place in range(chunk * half_slots, (chunk + 1) * half_slots):
            if place >= group:
                pltpu.make_async_remote_copy(
                    src_ref=stage.at[0],
                    dst_ref=here.at[slot_rows(place)],
                    send_sem=far_sems.at[0, place],
                    recv_sem=far_sems.at[1, place],
                    device_id={"col": col},
                    device_id_type=MESH,
                ).wait_recv()
            outs.append(put_out(here, current, place, 0))

        def split_here(i, carry):
            rows = pl.ds(pl.multiple_of(i * 32, 32), 32)
            top, low = split(here[pl.ds(pl.multiple_of(chunk * half_rows + i * 32, 32), 32), :])
            here_top[rows, :] = top
            here_low[rows, :] = low
            return carry

        lax.fori_loop(0, half_rows // 32, split_here, 0)

        def columns(i, carry):
            right = pl.ds(pl.multiple_of(i * tile, 128), tile)
            value = plain_nt(here_top[...], tops[right, :])
            value = value + plain_nt(here_top[...], lows[right, :])
            value = value + plain_nt(here_low[...], tops[right, :])
            projection[pl.ds(chunk * half_rows, half_rows), right] = value
            return carry

        lax.fori_loop(0, count * width // tile, columns, 0)

    def solve(reduce):
        value = jnp.concatenate([reduce.previous[i][...] for i in range(2)], axis=0)
        solved = None
        for panel in range(count - 1, -1, -1):
            term = value[:, panel * width : (panel + 1) * width]
            if solved is not None:
                rows = (count - 1 - panel) * width
                term = term - jnp.dot(
                    solved,
                    gram[pl.ds(starts[panel], rows), :],
                    precision=lax.Precision.HIGHEST,
                    preferred_element_type=jnp.float32,
                )
            piece = nt(term, factors[panel], lax.Precision.HIGHEST)
            solved = piece if solved is None else jnp.concatenate([piece, solved], axis=1)
        size = value.shape[0] // 2
        for i in range(2):
            reduce.place(i, solved[i * size : (i + 1) * size, :])

    def chunk_reduce(chunk, sems):
        rows = pl.ds(chunk * half_rows, half_rows)
        return Reduce(
            row, row_count, projection.at[rows], landing.at[chunk], solved_rows.at[rows], sems
        )

    late = list(steps[early:])
    inner = Reduce(row, row_count, partial, gram_landing, gram, gram_sems)
    stages = inner.count
    done = 0
    for number in range(stages):
        inner.halve_start(number)
        goal = len(late) * (number + 1) // stages
        for step in late[done:goal]:
            arrive(step)
        done = goal
        inner.halve_end()
    for i in range(2):
        inner.place(i, inner.previous[i][...])
    inner.double_start(0)
    project(0)
    inner.double_end()
    first = chunk_reduce(0, first_sems)
    for number in range(stages):
        first.halve_start(number)
        if number + 1 < stages:
            inner.double_start(number + 1)
            inner.double_end()
        first.halve_end()
    solve(first)
    first.double_start(0)
    project(1)
    first.double_end()
    second = chunk_reduce(1, second_sems)
    for number in range(stages):
        second.halve_start(number)
        if number + 1 < stages:
            first.double_start(number + 1)
            first.double_end()
        second.halve_end()
    for place in range(half_slots):
        outs.append(put_out(solved_rows, update, place, 1))
    solve(second)
    for number in range(stages):
        second.double_start(number)
        second.double_end()
    for place in range(half_slots, row_count):
        outs.append(put_out(solved_rows, update, place, 1))

    keep_panels.wait()
    for step in steps:
        sends[step].wait_send()
    for source_row in range(row_count):
        target, far = far_copy(source_row)

        @pl.when(target != col)
        def _():
            far.wait_send()

    for item in outs:
        item.wait()


def on_device(vectors, reflectors, factors):
    local_count, total_length = vectors.shape
    row_count = lax.axis_size("row")
    col_count = lax.axis_size("col")
    length = total_length // row_count
    count, part, _ = reflectors.shape
    width = part * col_count
    rows = local_count * row_count
    stages = len(strides_of(row_count))
    unit = 16 * row_count
    gram_rows = -(-(count * (count - 1) // 2 * width) // unit) * unit
    anywhere = pl.BlockSpec(memory_space=pl.ANY)
    vmem = pl.BlockSpec(memory_space=pltpu.VMEM)
    dma = pltpu.SemaphoreType.DMA
    single, half = jnp.float32, jnp.bfloat16
    current, panels, update = pl.pallas_call(
        functools.partial(kernel, row_count, col_count),
        name="exchange",
        out_shape=(
            jax.ShapeDtypeStruct((rows, length), single),
            jax.ShapeDtypeStruct((count * width, length), single),
            jax.ShapeDtypeStruct((rows, count * width), single),
        ),
        in_specs=[anywhere, anywhere, vmem],
        out_specs=(anywhere, anywhere, anywhere),
        scratch_shapes=[
            pltpu.VMEM((row_count, local_count, length), single),
            pltpu.VMEM((count * width, length), single),
            pltpu.VMEM((count * width, length), half),
            pltpu.VMEM((count * width, length), half),
            pltpu.VMEM((rows, length), single),
            pltpu.VMEM((rows // 2, length), half),
            pltpu.VMEM((rows // 2, length), half),
            pltpu.VMEM((rows, count * width), single),
            pltpu.VMEM((rows, count * width), single),
            pltpu.VMEM((2, 2, rows // 4, count * width), single),
            pltpu.VMEM((gram_rows, width), single),
            pltpu.VMEM((gram_rows, width), single),
            pltpu.VMEM((2, gram_rows // 2, width), single),
            dma((2, row_count)),
            dma((2, row_count)),
            dma((2, (col_count - 1) * count)),
            dma((1 + count,)),
            dma((2, row_count)),
            dma((2, 4 * stages)),
            dma((2, 4 * stages)),
            dma((2, 4 * stages)),
        ],
        compiler_params=pltpu.CompilerParams(
            collective_id=0, has_side_effects=True, vmem_limit_bytes=56 * 1024 * 1024
        ),
    )(vectors, reflectors, factors)
    return current - jnp.dot(update, panels, precision=HIGH, preferred_element_type=single)


def solution(mesh):
    return jax.shard_map(
        on_device,
        mesh=mesh,
        in_specs=(P(("row", "col"), None), P(None, "col", "row"), P()),
        out_specs=P("col", "row"),
        check_vma=False,
    )
```

profile of v0, /device:TPU:0, one launch (start us, length us, event | category | flops | bytes accessed | tf_op | source)
XLA Modules:
  0.0 178.1 jit_solution(10904458805690174483)
XLA Ops:
  0.0 168.3 %exchange.1 = (f32[512,2048]{1,0:T(8,128)}, f32[768,2048]{1,0:T(8,128)}, f32[512,768]{1,0:T(8,128)}) custom-call(f32[32,32768]{1,0:T(8,128)} %vectors.1, f32[6,64,2048]{2,1,0:T(8,128)} %reflectors.1, f32[6,128,128]{2,1,0:T(8,128)} %factors.1), custom_call_target="tpu_custom_call" | custom-call | tf_op jit(solution)/shard_map/exchange/pallas_call | solution.py:433
  168.4 9.7 %convolution_subtract_fusion = f32[512,2048]{1,0:T(8,128)} fusion(f32[512,2048]{1,0:T(8,128)} %get-tuple-element.8, f32[512,768]{1,0:T(8,128)} %get-tuple-element.9, f32[768,2048]{1,0:T(8,128)} %get-tuple-element.10), kind=kOutput, calls=%fused_computation | convolution fusion | flops 4832886784 | bytes 16252928 | tf_op jit(solution)/shard_map/dot_general | solution.py:470
where the time goes:
time: 178 us
  Pallas kernels  168 us (94%)
  matrix products  9.74 us (5%)
    pallas_call x1, Pallas kernels, on_device(): pl.pallas_call(functools.partial(kernel, row_count, col_count), name='exc...  168 us
    dot_general x1, matrix products, on_device(): jnp.dot(update, panels, precision=HIGH, preferred_element_type=single)  9.74 us

commit v1 on v0

v1 whole, which is shorter than its diff:
```python
import functools

import jax
import jax.numpy as jnp
from jax import lax
from jax.experimental import pallas as pl
from jax.experimental.pallas import tpu as pltpu
from jax.sharding import PartitionSpec as P

MESH = pl.DeviceIdType.MESH
HIGHEST = lax.Precision.HIGHEST
SUB = 8


def nt(left, right, precision=None):
    return lax.dot_general(
        left,
        right,
        (((1,), (1,)), ((), ())),
        precision=precision,
        preferred_element_type=jnp.float32,
    )


def nn(left, right, precision=None):
    return jnp.dot(left, right, precision=precision, preferred_element_type=jnp.float32)


def split(value):
    top = value.astype(jnp.bfloat16)
    return top, (value - top.astype(jnp.float32)).astype(jnp.bfloat16)


def doubled(value, width):
    columns = value.shape[1]
    pieces = []
    for part in split(value):
        twice = []
        for start in range(0, columns, width):
            piece = part[:, start : start + width]
            twice += [piece, piece]
        pieces.append(jnp.concatenate(twice, axis=1))
    return jnp.concatenate(pieces, axis=0)


def bits_of(count):
    return count.bit_length() - 1


def bit(value, stride):
    return (value // stride) % 2


def mirrored(value, bits):
    found = 0
    for i in range(bits):
        found = found + bit(value, 1 << i) * (1 << (bits - 1 - i))
    return found


class Chain:
    def __init__(self, steps):
        self.steps = list(steps)
        self.open = None

    def tick(self):
        if self.open is not None:
            self.open()
            self.open = None
        if self.steps:
            start, end = self.steps.pop(0)
            start()
            self.open = end


def tick(*chains):
    for chain in chains:
        if chain.open is not None:
            chain.open()
            chain.open = None
    for chain in chains:
        chain.tick()


def kernel(
    row_count, col_count, vectors, reflectors, factors, out,
    stage, here, held, both, mixed, projection, landing, wide, solved, weights,
    system, pairs, partial, gram_landing, gram,
    row_sems, local_sems, gather_sems, far_sems, sum_sems, cross_sems, wide_sems,
    gram_sems, out_sems,
):
    row = lax.axis_index("row")
    col = lax.axis_index("col")
    chunks = stage.shape[0]
    local = chunks * SUB
    length = held.shape[1]
    count, part, _ = reflectors.shape
    width = part * col_count
    group = row_count // col_count
    row_bits, col_bits, group_bits = bits_of(row_count), bits_of(col_count), bits_of(group)
    rows = row_count * SUB
    high, low = row // group, row % group
    my_place = mirrored(low, group_bits)

    barrier = pltpu.get_barrier_semaphore()
    for step in range(1, row_count):
        pl.semaphore_signal(
            barrier, inc=1, device_id={"row": lax.rem(row + step, row_count)}, device_id_type=MESH
        )
    for step in range(1, col_count):
        pl.semaphore_signal(
            barrier, inc=1, device_id={"col": lax.rem(col + step, col_count)}, device_id_type=MESH
        )
    pairing = [
        (dh, dc) for dh in range(1, col_count) for dc in range(1, col_count)
    ]
    for dh, dc in pairing:
        pl.semaphore_signal(
            barrier,
            inc=1,
            device_id={
                "row": lax.rem(high + dh, col_count) * group + low,
                "col": lax.rem(col + dc, col_count),
            },
            device_id_type=MESH,
        )
    pl.semaphore_wait(barrier, row_count + col_count - 2 + len(pairing))

    def remote(source, target, sems, number, device, arrival=None):
        return pltpu.make_async_remote_copy(
            src_ref=source,
            dst_ref=target,
            send_sem=sems.at[0, number],
            recv_sem=sems.at[1, number if arrival is None else arrival],
            device_id=device,
            device_id_type=MESH,
        )

    order = list(range(count - 1, -1, -1))
    gathers = {}
    for panel in order:
        place = held.at[pl.ds(pl.multiple_of(panel * width + col * part, SUB), part)]
        gathers[panel] = []
        for step in range(1, col_count):
            item = remote(
                reflectors.at[panel], place, gather_sems, (step - 1) * count + panel,
                {"col": lax.rem(col + step, col_count)},
            )
            item.start()
            gathers[panel].append(item)
    for panel in order:
        place = held.at[pl.ds(pl.multiple_of(panel * width + col * part, SUB), part)]
        item = pltpu.make_async_copy(reflectors.at[panel], place, local_sems.at[panel])
        item.start()
        gathers[panel].append(item)

    middle = row_count // 2
    ranked = sorted(range(1, row_count), key=lambda step: (abs(step - middle), step))
    steps = []
    while ranked:
        steps.append(ranked.pop(0))
        if ranked:
            steps.append(ranked.pop())
    arrivals = {}

    def send_rows(chunk):
        place = stage.at[
            chunk, my_place,
            pl.ds(pl.multiple_of(mirrored(high, col_bits) * SUB, SUB), SUB),
        ]
        taken = pl.ds(chunk * SUB, SUB)
        items = []
        for step in steps:
            other = lax.rem(row + step, row_count)
            item = remote(
                vectors.at[taken, pl.ds(pl.multiple_of(other * length, 128), length)],
                place, row_sems, chunk * row_count + step, {"row": other},
            )
            item.start()
            items.append(item)
        item = pltpu.make_async_copy(
            vectors.at[taken, pl.ds(pl.multiple_of(row * length, 128), length)],
            place, local_sems.at[count + chunk],
        )
        item.start()
        items.append(item)
        arrivals[chunk] = items

    for chunk in range(chunks):
        send_rows(chunk)

    def take_rows(chunk):
        for item in arrivals[chunk]:
            item.wait()
        own = pl.ds(pl.multiple_of(mirrored(col, col_bits) * SUB, SUB), SUB)
        mine = pl.ds(pl.multiple_of(col * SUB, SUB), SUB)
        size = col_count * SUB

        def body(i, carry):
            top, low_part = split(stage[chunk, i])
            at = pl.multiple_of(i * size, size)
            mixed[chunk, pl.ds(at, size), :] = top
            mixed[chunk, pl.ds(pl.multiple_of(rows + at, size), size), :] = low_part
            here[chunk, i, mine, :] = stage[chunk, i, own, :]
            return carry

        lax.fori_loop(0, group, body, 0)

    def take_panel(panel):
        for item in gathers[panel]:
            item.wait()

        def body(i, carry):
            at = pl.multiple_of(panel * width + i * 32, 32)
            top, low_part = split(held[pl.ds(at, 32), :])
            to = pl.multiple_of(2 * panel * width + i * 32, 32)
            both[pl.ds(to, 32), :] = top
            both[pl.ds(pl.multiple_of(to + width, 32), 32), :] = low_part
            return carry

        lax.fori_loop(0, width // 32, body, 0)

    def panel_rows(panel):
        return pl.ds(pl.multiple_of(2 * panel * width, 2 * width), 2 * width)

    def quadrants(value, above, left):
        value = value[:above] + value[above:]
        return value[:, :left] + value[:, left:]

    bases = {}
    base = 0
    for panel in range(count - 2, -1, -1):
        bases[panel] = base
        base += (count - 1 - panel) * width

    def inner(panel):
        def body(i, carry):
            value = nt(both[panel_rows(panel + 1 + i), :], both[panel_rows(panel), :])
            to = pl.multiple_of(bases[panel] + i * width, width)
            partial[pl.ds(to, width), :] = quadrants(value, width, width)
            return carry

        if panel < count - 1:
            lax.fori_loop(0, count - 1 - panel, body, 0)

    def project(chunk, first, last):
        def body(i, carry):
            value = nt(mixed[chunk], both[panel_rows(first + i), :])
            to = pl.ds(pl.multiple_of((first + i) * width, width), width)
            projection[chunk, :, to] = quadrants(value, rows, width)
            return carry

        lax.fori_loop(0, last - first, body, 0)

    def halving(source, target, sems, number):
        total = source.shape[0]
        state = {"now": source}
        steps = []
        for stage_number in range(row_bits):
            stride = 1 << stage_number
            half = total >> (stage_number + 1)
            start = total - (total >> stage_number)

            def begin(stride=stride, half=half, start=start, stage_number=stage_number):
                away = pl.ds(pl.multiple_of((1 - bit(row, stride)) * half, SUB), half)
                place = target.at[pl.ds(start, half)]
                item = remote(
                    state["now"].at[away], place, sems, number + stage_number,
                    {"row": row + stride * (1 - 2 * bit(row, stride))},
                )
                item.start()
                state["item"], state["place"] = item, place

            def end(stride=stride, half=half):
                state["item"].wait()
                keep = pl.ds(pl.multiple_of(bit(row, stride) * half, SUB), half)
                place = state["place"]
                place[...] = place[...] + state["now"][keep, :]
                state["now"] = place

            steps.append((begin, end))
        return Chain(steps), state

    def doubling(strides, target, sems, number, position, size):
        state = {"position": position, "size": size}
        steps = []
        for stage_number, stride in enumerate(strides):
            def begin(stride=stride, stage_number=stage_number):
                where = target.at[pl.ds(state["position"], state["size"])]
                item = remote(
                    where, where, sems, number + stage_number,
                    {"row": row + stride * (1 - 2 * bit(row, stride))},
                )
                item.start()
                state["item"] = item

            def end(stride=stride):
                state["item"].wait()
                state["position"] = state["position"] - bit(row, stride) * state["size"]
                state["size"] = state["size"] * 2

            steps.append((begin, end))
        return steps

    def cross(chunk):
        rows_of = pl.ds(pl.multiple_of(col * SUB, SUB), SUB)
        items = []
        base = chunk * col_count

        def begin():
            place = wide.at[chunk, my_place, rows_of]
            for step in range(col_count):
                other = lax.rem(high + step, col_count)
                item = remote(
                    solved.at[chunk], place, cross_sems, base + step,
                    {"row": other * group + low, "col": high}, base + col,
                )
                items.append(item)
                if step:
                    item.start()

            @pl.when(col != high)
            def _():
                items[0].start()

            @pl.when(col == high)
            def _():
                wide[chunk, my_place, rows_of, :] = solved[chunk]

        def end():
            for step in range(1, col_count):
                items[step].wait_send()

            @pl.when(col != high)
            def _():
                items[0].wait_send()

            for other in range(col_count):
                item = remote(
                    solved.at[chunk],
                    wide.at[chunk, my_place, pl.ds(other * SUB, SUB)],
                    cross_sems, base, {"row": row, "col": col}, base + other,
                )

                @pl.when((col != high) | (col != other))
                def _():
                    item.wait_recv()

        return begin, end

    def spread(chunk):
        strides = [group >> (i + 1) for i in range(group_bits)]
        return Chain(
            [cross(chunk)]
            + doubling(strides, wide.at[chunk], wide_sems, chunk * max(group_bits, 1), my_place, 1)
        )

    far = {}

    def send_far(chunk):
        items = []
        for step in range(1, col_count):
            other = lax.rem(col + step, col_count)
            source = pl.ds(pl.multiple_of(mirrored(other, col_bits) * SUB, SUB), SUB)
            target = pl.ds(pl.multiple_of(col * SUB, SUB), SUB)
            item = remote(
                stage.at[chunk, :, source], here.at[chunk, :, target],
                far_sems, chunk * col_count + step, {"col": other},
            )
            item.start()
            items.append(item)
        far[chunk] = items

    def build():
        system[...] = jnp.zeros_like(system)
        for panel in range(count - 1, -1, -1):
            at = pl.ds(panel * width, width)
            system[at, at] = factors[panel].T
            if panel < count - 1:
                below = pl.ds((panel + 1) * width, (count - 1 - panel) * width)
                value = nn(
                    system[below, below], gram[pl.ds(bases[panel], below.size), :], HIGHEST
                )
                system[below, at] = -nt(value, factors[panel], HIGHEST)
        for panel in range(count):
            top, low_part = split(system[pl.ds(panel * width, width), :])
            pairs[pl.ds(2 * panel * width, width), :] = top
            pairs[pl.ds((2 * panel + 1) * width, width), :] = low_part

    def solve(states, numbers):
        value = jnp.concatenate([states[number]["now"][...] for number in numbers], axis=0)
        size = value.shape[0]
        value = nn(doubled(value, width), pairs[...])
        value = value[:size] + value[size:]
        for i, number in enumerate(numbers):
            solved[number] = value[i * SUB : (i + 1) * SUB]

    outs = []
    tile = 512 if length % 512 == 0 else length

    def update(chunk):
        for item in far[chunk]:
            item.wait()
        weights[...] = doubled(wide[chunk].reshape(rows, count * width), width)

        def body(i, carry):
            at = pl.ds(pl.multiple_of(i * tile, tile), tile)
            value = nn(weights[...], both[:, at])
            value = (value[:rows] + value[rows:]).reshape(group, col_count * SUB, tile)
            here[chunk, :, :, at] = here[chunk, :, :, at] - value
            return carry

        lax.fori_loop(0, length // tile, body, 0)
        for place in range(group):
            for other in range(col_count):
                slot = mirrored(place, group_bits) * col_count + other
                item = pltpu.make_async_copy(
                    here.at[chunk, place, pl.ds(other * SUB, SUB)],
                    out.at[pl.ds(slot * local + chunk * SUB, SUB)],
                    out_sems.at[chunk * row_count + place * col_count + other],
                )
                item.start()
                outs.append(item)

    due = [((chunk + 1) / chunks, 1, chunk) for chunk in range(chunks - 1)]
    due += [(0.78 * (i + 1) / count, 0, panel) for i, panel in enumerate(order)]
    ready_rows, done = [], {}
    lowest = count
    for _, kind, number in sorted(due):
        if kind == 0:
            take_panel(number)
            inner(number)
            lowest = number
        else:
            take_rows(number)
            ready_rows.append(number)
            done[number] = count
        last = number == 0 and kind == 0
        for chunk in ready_rows:
            if done[chunk] - lowest >= 2 or (lowest == 0 and done[chunk] > 0):
                project(chunk, lowest, done[chunk])
                done[chunk] = lowest
    early = list(range(chunks - 1))
    late = chunks - 1
    for chunk in early:
        send_far(chunk)
    sums = {}
    states = {}
    for chunk in range(chunks):
        sums[chunk], states[chunk] = halving(
            projection.at[chunk], landing.at[chunk], sum_sems, chunk * row_bits
        )
    gram_rows = gram.shape[0]
    used = bases[0] + (count - 1) * width
    if used < gram_rows:
        partial[pl.ds(used, gram_rows - used), :] = jnp.zeros((gram_rows - used, width), jnp.float32)
    gram_chain, gram_state = halving(partial, gram_landing, gram_sems, 0)
    first = [sums[chunk] for chunk in early]
    tick(gram_chain, *first)
    for number in range(row_bits):
        tick(gram_chain, *first)
    piece = gram_rows // row_count
    place = mirrored(row, row_bits) * piece
    gram[pl.ds(pl.multiple_of(place, SUB), piece), :] = gram_state["now"][...]
    strides = [1 << i for i in range(row_bits - 1, -1, -1)]
    gram_chain = Chain(
        doubling(strides, gram, gram_sems, row_bits, pl.multiple_of(place, SUB), piece)
    )
    tick(gram_chain)
    for number in range(row_bits - 2):
        tick(gram_chain)
    take_rows(late)
    send_far(late)
    project(late, 0, count)
    tick(gram_chain, sums[late])
    tick(gram_chain)
    build()
    solve(states, early)
    spreads = {chunk: spread(chunk) for chunk in range(chunks)}
    first = [spreads[chunk] for chunk in early]
    for number in range(row_bits):
        tick(sums[late], *first)
    solve(states, [late])
    tick(spreads[late], *first)
    for number in range(max(group_bits - row_bits, 0)):
        tick(*first)
    for chunk in early[:-1]:
        update(chunk)
    tick(spreads[late])
    if early:
        update(early[-1])
    for number in range(group_bits):
        tick(spreads[late])
    update(late)
    for item in outs:
        item.wait()


def on_device(vectors, reflectors, factors):
    local, total_length = vectors.shape
    row_count = lax.axis_size("row")
    col_count = lax.axis_size("col")
    length = total_length // row_count
    count, part, _ = reflectors.shape
    width = part * col_count
    every = count * width
    chunks = local // SUB
    group = row_count // col_count
    row_bits, group_bits = bits_of(row_count), bits_of(group)
    rows = row_count * SUB
    unit = SUB * row_count
    gram_rows = -(-(count * (count - 1) // 2 * width) // unit) * unit
    anywhere = pl.BlockSpec(memory_space=pl.ANY)
    vmem = pl.BlockSpec(memory_space=pltpu.VMEM)
    dma = pltpu.SemaphoreType.DMA
    single, half = jnp.float32, jnp.bfloat16
    return pl.pallas_call(
        functools.partial(kernel, row_count, col_count),
        name="exchange",
        out_shape=jax.ShapeDtypeStruct((local * row_count, length), single),
        in_specs=[anywhere, anywhere, vmem],
        out_specs=anywhere,
        scratch_shapes=[
            pltpu.VMEM((chunks, group, col_count * SUB, length), single),
            pltpu.VMEM((chunks, group, col_count * SUB, length), single),
            pltpu.VMEM((every, length), single),
            pltpu.VMEM((2 * every, length), half),
            pltpu.VMEM((chunks, 2 * rows, length), half),
            pltpu.VMEM((chunks, rows, every), single),
            pltpu.VMEM((chunks, rows, every), single),
            pltpu.VMEM((chunks, group, col_count * SUB, every), single),
            pltpu.VMEM((chunks, SUB, every), single),
            pltpu.VMEM((2 * rows, 2 * every), half),
            pltpu.VMEM((every, every), single),
            pltpu.VMEM((2 * every, every), half),
            pltpu.VMEM((gram_rows, width), single),
            pltpu.VMEM((gram_rows, width), single),
            pltpu.VMEM((gram_rows, width), single),
            dma((2, chunks * row_count)),
            dma((count + chunks,)),
            dma((2, (col_count - 1) * count)),
            dma((2, chunks * col_count)),
            dma((2, chunks * row_bits)),
            dma((2, chunks * col_count)),
            dma((2, chunks * max(group_bits, 1))),
            dma((2, 2 * row_bits)),
            dma((chunks * row_count,)),
        ],
        compiler_params=pltpu.CompilerParams(
            collective_id=0, has_side_effects=True, vmem_limit_bytes=60 * 1024 * 1024
        ),
    )(vectors, reflectors, factors)


def solution(mesh):
    return jax.shard_map(
        on_device,
        mesh=mesh,
        in_specs=(P(("row", "col"), None), P(None, "col", "row"), P()),
        out_specs=P("col", "row"),
        check_vma=False,
    )
```

time: 178 us -> 191 us (1.073)
  Pallas kernels: 168 us -> 186 us
  matrix products: 9.74 us -> 0 us
  local copies, waits for them, and re-layouts: 0 us -> 4.7 us
    pallas_call x1, Pallas kernels: 168 us -> 186 us  [on_device(): pl.pallas_call(functools.partial(kernel, row_count, col_count), name='exc...]
    dot_general x1 -> x0, matrix products: 9.74 us -> none  [on_device(): jnp.dot(update, panels, precision=HIGH, preferred_element_type=single)]
    unnamed x0 -> x1, local copies, waits for them, and re-layouts: none -> 4.7 us
where the time goes in v1:
time: 191 us; the launch traced here: 190 us
  Pallas kernels  186 us (97%)
  local copies, waits for them, and re-layouts  4.7 us (2%)
    pallas_call x1, Pallas kernels, on_device(): pl.pallas_call(functools.partial(kernel, row_count, col_count), name='exc...  186 us
    unnamed x1, local copies, waits for them, and re-layouts  4.7 us

profile of v1, /device:TPU:0, one launch (start us, length us, event | category | flops | bytes accessed | tf_op | source)
XLA Modules:
  0.0 190.5 jit_solution(11946261223799051288)
XLA Ops:
  0.0 185.8 %exchange.1 = f32[512,2048]{1,0:T(8,128)} custom-call(f32[32,32768]{1,0:T(8,128)} %vectors.1, f32[6,64,2048]{2,1,0:T(8,128)} %reflectors.1, f32[6,128,128]{2,1,0:T(8,128)} %factors.1), custom_call_target="tpu_custom_call" | custom-call | tf_op jit(solution)/shard_map/exchange/pallas_call | solution.py:517
  185.8 4.7 %copy.5 = f32[512,2048]{1,0:T(8,128)} copy(f32[512,2048]{1,0:T(8,128)} %exchange.1) | data formatting | bytes 8388608

commit v2 on v1

--- a/solution.py
+++ b/solution.py
@@ -10,6 +10,10 @@
 MESH = pl.DeviceIdType.MESH
 HIGHEST = lax.Precision.HIGHEST
 SUB = 8
+WIDER = -5
+GAP0 = 0.025
+GAP = 0.1
+AFTER = 0
 
 
 def nt(left, right, precision=None):
@@ -58,10 +62,28 @@
     return found
 
 
+def batches(count):
+    found = [list(range(count - 2, 1, -1)), [1], [0]]
+    return [[panel for panel in panels if panel < count - 1] for panels in found if panels]
+
+
+def padded(size, row_count):
+    unit = SUB * row_count
+    return -(-size // unit) * unit
+
+
 class Chain:
     def __init__(self, steps):
         self.steps = list(steps)
         self.open = None
+        self.due = 0.0
+        self.made = 0
+
+    def tick_at(self, time):
+        if time >= self.due:
+            self.tick()
+            self.due = time + (GAP0 if self.made == 0 else GAP)
+            self.made += 1
 
     def tick(self):
         if self.open is not None:
@@ -75,11 +97,11 @@
 
 def tick(*chains):
     for chain in chains:
-        if chain.open is not None:
-            chain.open()
-            chain.open = None
-    for chain in chains:
         chain.tick()
+
+
+def busy(*chains):
+    return any(chain.open is not None or chain.steps for chain in chains)
 
 
 def kernel(
@@ -161,37 +183,41 @@
         steps.append(ranked.pop(0))
         if ranked:
             steps.append(ranked.pop())
-    arrivals = {}
-
-    def send_rows(chunk):
-        place = stage.at[
-            chunk, my_place,
-            pl.ds(pl.multiple_of(mirrored(high, col_bits) * SUB, SUB), SUB),
-        ]
-        taken = pl.ds(chunk * SUB, SUB)
-        items = []
+    place = stage.at[
+        :, my_place, pl.ds(pl.multiple_of(mirrored(high, col_bits) * SUB, SUB), SUB)
+    ]
+    sends = []
+    for chunk in range(chunks):
         for step in steps:
             other = lax.rem(row + step, row_count)
             item = remote(
-                vectors.at[taken, pl.ds(pl.multiple_of(other * length, 128), length)],
-                place, row_sems, chunk * row_count + step, {"row": other},
+                vectors.at[
+                    pl.ds(chunk * SUB, SUB), pl.ds(pl.multiple_of(other * length, 128), length)
+                ],
+                place.at[chunk], row_sems, chunk * row_count + step, {"row": other},
             )
-            item.start()
-            items.append(item)
+            sends.append(item)
+    own_rows = []
+    for chunk in range(chunks):
         item = pltpu.make_async_copy(
-            vectors.at[taken, pl.ds(pl.multiple_of(row * length, 128), length)],
-            place, local_sems.at[count + chunk],
+            vectors.at[
+                pl.ds(chunk * SUB, SUB), pl.ds(pl.multiple_of(row * length, 128), length)
+            ],
+            place.at[chunk], local_sems.at[count + chunk],
         )
         item.start()
-        items.append(item)
-        arrivals[chunk] = items
-
-    for chunk in range(chunks):
-        send_rows(chunk)
+        own_rows.append(item)
+    window = len(steps) + WIDER
+    for item in sends[:window]:
+        item.start()
+
+    def arrive(number):
+        sends[number].wait()
+        if number + window < len(sends):
+            sends[number + window].start()
 
     def take_rows(chunk):
-        for item in arrivals[chunk]:
-            item.wait()
+        own_rows[chunk].wait()
         own = pl.ds(pl.multiple_of(mirrored(col, col_bits) * SUB, SUB), SUB)
         mine = pl.ds(pl.multiple_of(col * SUB, SUB), SUB)
         size = col_count * SUB
@@ -227,11 +253,18 @@
         value = value[:above] + value[above:]
         return value[:, :left] + value[:, left:]
 
-    bases = {}
+    bases, bounds = {}, []
     base = 0
-    for panel in range(count - 2, -1, -1):
-        bases[panel] = base
-        base += (count - 1 - panel) * width
+    for panels in batches(count):
+        first = base
+        for panel in panels:
+            bases[panel] = base
+            base += (count - 1 - panel) * width
+        used = base
+        base = first + padded(used - first, row_count)
+        if used < base:
+            partial[pl.ds(used, base - used), :] = jnp.zeros((base - used, width), jnp.float32)
+        bounds.append((first, base - first))
 
     def inner(panel):
         def body(i, carry):
@@ -371,37 +404,28 @@
             items.append(item)
         far[chunk] = items
 
-    def build():
-        system[...] = jnp.zeros_like(system)
-        for panel in range(count - 1, -1, -1):
-            at = pl.ds(panel * width, width)
-            system[at, at] = factors[panel].T
-            if panel < count - 1:
-                below = pl.ds((panel + 1) * width, (count - 1 - panel) * width)
-                value = nn(
-                    system[below, below], gram[pl.ds(bases[panel], below.size), :], HIGHEST
-                )
-                system[below, at] = -nt(value, factors[panel], HIGHEST)
+    def build(panel):
+        at = pl.ds(panel * width, width)
+        system[at, at] = factors[panel].T
+        if panel < count - 1:
+            below = pl.ds((panel + 1) * width, (count - 1 - panel) * width)
+            value = nn(system[below, below], gram[pl.ds(bases[panel], below.size), :], HIGHEST)
+            system[below, at] = -nt(value, factors[panel], HIGHEST)
+
+    def finish():
         for panel in range(count):
             top, low_part = split(system[pl.ds(panel * width, width), :])
             pairs[pl.ds(2 * panel * width, width), :] = top
             pairs[pl.ds((2 * panel + 1) * width, width), :] = low_part
 
-    def solve(states, numbers):
-        value = jnp.concatenate([states[number]["now"][...] for number in numbers], axis=0)
-        size = value.shape[0]
-        value = nn(doubled(value, width), pairs[...])
-        value = value[:size] + value[size:]
-        for i, number in enumerate(numbers):
-            solved[number] = value[i * SUB : (i + 1) * SUB]
-
     outs = []
     tile = 512 if length % 512 == 0 else length
 
     def update(chunk):
         for item in far[chunk]:
             item.wait()
-        weights[...] = doubled(wide[chunk].reshape(rows, count * width), width)
+        value = nn(doubled(wide[chunk].reshape(rows, count * width), width), pairs[...])
+        weights[...] = doubled(value[:rows] + value[rows:], width)
 
         def body(i, carry):
             at = pl.ds(pl.multiple_of(i * tile, tile), tile)
@@ -422,75 +446,153 @@
                 item.start()
                 outs.append(item)
 
-    due = [((chunk + 1) / chunks, 1, chunk) for chunk in range(chunks - 1)]
-    due += [(0.78 * (i + 1) / count, 0, panel) for i, panel in enumerate(order)]
-    ready_rows, done = [], {}
-    lowest = count
-    for _, kind, number in sorted(due):
-        if kind == 0:
+    system[...] = jnp.zeros_like(system)
+
+    row_chains, gram_chains = {chunk: [] for chunk in range(chunks)}, []
+    pieces = {chunk: [] for chunk in range(chunks)}
+    sum_count, gram_count = [0], [0]
+
+    def sum_rows(chunk, first, last):
+        columns = pl.ds(first * width, (last - first) * width)
+        chain, state = halving(
+            projection.at[chunk, :, columns], landing.at[chunk, :, columns], sum_sems,
+            sum_count[0] * row_bits,
+        )
+        sum_count[0] += 1
+        pieces[chunk].append((columns, state))
+        row_chains[chunk].append(chain)
+        return chain
+
+    def sum_gram(number):
+        first, size = bounds[number]
+        piece = size // row_count
+        place = mirrored(row, row_bits) * piece
+        target = gram.at[pl.ds(first, size)]
+        base = gram_count[0] * 2 * row_bits
+        gram_count[0] += 1
+        chain, state = halving(
+            partial.at[pl.ds(first, size)], gram_landing.at[pl.ds(first, size)], gram_sems, base
+        )
+
+        def put():
+            target[pl.ds(pl.multiple_of(place, SUB), piece), :] = state["now"][...]
+
+        strides = [1 << i for i in range(row_bits - 1, -1, -1)]
+        later = doubling(
+            strides, target, gram_sems, base + row_bits, pl.multiple_of(place, SUB), piece
+        )
+        begin, end = later[0]
+
+        def put_and_begin():
+            put()
+            begin()
+
+        chain.steps += [(put_and_begin, end)] + later[1:]
+        gram_chains.append(chain)
+        return chain
+
+    def gather(chunk):
+        chain = spread(chunk)
+        begin, end = chain.steps[0]
+
+        def join_and_begin():
+            for columns, state in pieces[chunk]:
+                solved[chunk, :, columns] = state["now"][...]
+            begin()
+
+        chain.steps[0] = (join_and_begin, end)
+        return chain
+
+    per = len(steps)
+    late = chunks - 1
+    due = [((number + 1) / len(sends), 2, number) for number in range(len(sends) - per)]
+    due += [(0.04 + 0.124 * (i + 1) * 6 / count, 1, panel) for i, panel in enumerate(order)]
+    groups = batches(count)
+    closing = {panels[-1]: number for number, panels in enumerate(groups) if panels}
+    chains, taken, started = [], [], {}
+    for time, kind, number in sorted(due):
+        for chain in chains:
+            chain.tick_at(time)
+        if kind == 2:
+            arrive(number)
+            if (number + 1) % per == 0:
+                chunk = number // per
+                take_rows(chunk)
+                taken.append(chunk)
+                started[chunk] = count
+        else:
             take_panel(number)
+            if number == 0:
+                for chunk in taken:
+                    send_far(chunk)
             inner(number)
-            lowest = number
-        else:
-            take_rows(number)
-            ready_rows.append(number)
-            done[number] = count
-        last = number == 0 and kind == 0
-        for chunk in ready_rows:
-            if done[chunk] - lowest >= 2 or (lowest == 0 and done[chunk] > 0):
-                project(chunk, lowest, done[chunk])
-                done[chunk] = lowest
-    early = list(range(chunks - 1))
-    late = chunks - 1
-    for chunk in early:
-        send_far(chunk)
-    sums = {}
-    states = {}
-    for chunk in range(chunks):
-        sums[chunk], states[chunk] = halving(
-            projection.at[chunk], landing.at[chunk], sum_sems, chunk * row_bits
-        )
-    gram_rows = gram.shape[0]
-    used = bases[0] + (count - 1) * width
-    if used < gram_rows:
-        partial[pl.ds(used, gram_rows - used), :] = jnp.zeros((gram_rows - used, width), jnp.float32)
-    gram_chain, gram_state = halving(partial, gram_landing, gram_sems, 0)
-    first = [sums[chunk] for chunk in early]
-    tick(gram_chain, *first)
-    for number in range(row_bits):
-        tick(gram_chain, *first)
-    piece = gram_rows // row_count
-    place = mirrored(row, row_bits) * piece
-    gram[pl.ds(pl.multiple_of(place, SUB), piece), :] = gram_state["now"][...]
-    strides = [1 << i for i in range(row_bits - 1, -1, -1)]
-    gram_chain = Chain(
-        doubling(strides, gram, gram_sems, row_bits, pl.multiple_of(place, SUB), piece)
-    )
-    tick(gram_chain)
-    for number in range(row_bits - 2):
-        tick(gram_chain)
+            if number in closing:
+                ready = [chunk for chunk in taken if started[chunk] > number]
+                for chunk in ready:
+                    project(chunk, number, started[chunk])
+                fresh = [sum_rows(chunk, number, started[chunk]) for chunk in ready]
+                for chunk in ready:
+                    started[chunk] = number
+                fresh.append(sum_gram(closing[number]))
+                for chain in fresh:
+                    chain.tick_at(time)
+                chains += fresh
+    for chunk in range(late):
+        if chunk not in far:
+            send_far(chunk)
+        if started[chunk] > 0:
+            project(chunk, 0, started[chunk])
+            chain = sum_rows(chunk, 0, started[chunk])
+            chain.tick()
+            chains.append(chain)
+    built = [count]
+
+    def build_ready():
+        for number, panels in enumerate(groups):
+            if number < len(groups) and not busy(gram_chains[number]):
+                lowest = panels[-1] if panels else count - 1
+                for panel in range(built[0] - 1, lowest - 1, -1):
+                    build(panel)
+                    built[0] = panel
+            else:
+                break
+
+    spreads = {}
+
+    def gather_ready():
+        for chunk in range(late):
+            if chunk not in spreads and not busy(*row_chains[chunk]):
+                spreads[chunk] = gather(chunk)
+                spreads[chunk].tick()
+
+    for number in range(AFTER):
+        tick(*chains)
+    for number in range(late * per, len(sends)):
+        arrive(number)
     take_rows(late)
     send_far(late)
     project(late, 0, count)
-    tick(gram_chain, sums[late])
-    tick(gram_chain)
-    build()
-    solve(states, early)
-    spreads = {chunk: spread(chunk) for chunk in range(chunks)}
-    first = [spreads[chunk] for chunk in early]
-    for number in range(row_bits):
-        tick(sums[late], *first)
-    solve(states, [late])
-    tick(spreads[late], *first)
-    for number in range(max(group_bits - row_bits, 0)):
-        tick(*first)
-    for chunk in early[:-1]:
+    final = sum_rows(late, 0, count)
+    final.tick()
+    while busy(final):
+        tick(*chains, *spreads.values())
+        gather_ready()
+        build_ready()
+        final.tick()
+    final = gather(late)
+    final.tick()
+    while busy(*chains) or len(spreads) < late or busy(*spreads.values()):
+        tick(*chains, *spreads.values())
+        gather_ready()
+        build_ready()
+        final.tick()
+    build_ready()
+    finish()
+    for chunk in range(late):
         update(chunk)
-    tick(spreads[late])
-    if early:
-        update(early[-1])
-    for number in range(group_bits):
-        tick(spreads[late])
+        final.tick()
+    while busy(final):
+        final.tick()
     update(late)
     for item in outs:
         item.wait()
@@ -508,8 +610,10 @@
     group = row_count // col_count
     row_bits, group_bits = bits_of(row_count), bits_of(group)
     rows = row_count * SUB
-    unit = SUB * row_count
-    gram_rows = -(-(count * (count - 1) // 2 * width) // unit) * unit
+    gram_rows = 0
+    for panels in batches(count):
+        used = sum((count - 1 - panel) * width for panel in panels)
+        gram_rows += padded(used, row_count)
     anywhere = pl.BlockSpec(memory_space=pl.ANY)
     vmem = pl.BlockSpec(memory_space=pltpu.VMEM)
     dma = pltpu.SemaphoreType.DMA
@@ -540,10 +644,10 @@
             dma((count + chunks,)),
             dma((2, (col_count - 1) * count)),
             dma((2, chunks * col_count)),
-            dma((2, chunks * row_bits)),
+            dma((2, 3 * chunks * row_bits)),
             dma((2, chunks * col_count)),
             dma((2, chunks * max(group_bits, 1))),
-            dma((2, 2 * row_bits)),
+            dma((2, 3 * 2 * row_bits)),
             dma((chunks * row_count,)),
         ],
         compiler_params=pltpu.CompilerParams(

time: 191 us -> 167 us (0.87)
  Pallas kernels: 186 us -> 161 us
    pallas_call x1, Pallas kernels: 186 us -> 161 us  [on_device(): pl.pallas_call(functools.partial(kernel, row_count, col_count), name='exc...]
where the time goes in v2:
time: 167 us; the launch traced here: 166 us
  Pallas kernels  161 us (96%)
  local copies, waits for them, and re-layouts  4.7 us (3%)
    pallas_call x1, Pallas kernels, on_device(): pl.pallas_call(functools.partial(kernel, row_count, col_count), name='exc...  161 us
    unnamed x1, local copies, waits for them, and re-layouts  4.7 us

profile of v2, /device:TPU:0, one launch (start us, length us, event | category | flops | bytes accessed | tf_op | source)
XLA Modules:
  0.0 165.7 jit_solution(10688074227093621460)
XLA Ops:
  0.0 161.0 %exchange.1 = f32[512,2048]{1,0:T(8,128)} custom-call(f32[32,32768]{1,0:T(8,128)} %vectors.1, f32[6,64,2048]{2,1,0:T(8,128)} %reflectors.1, f32[6,128,128]{2,1,0:T(8,128)} %factors.1), custom_call_target="tpu_custom_call" | custom-call | tf_op jit(solution)/shard_map/exchange/pallas_call | solution.py:621
  161.0 4.7 %copy.5 = f32[512,2048]{1,0:T(8,128)} copy(f32[512,2048]{1,0:T(8,128)} %exchange.1) | data formatting | bytes 8388608

commit v3 on v2

--- a/solution.py
+++ b/solution.py
@@ -12,8 +12,9 @@
 SUB = 8
 WIDER = -5
 GAP0 = 0.025
-GAP = 0.1
-AFTER = 0
+GAP = 0.12
+TURNED = (1,)
+GRAM_TURNED = ()
 
 
 def nt(left, right, precision=None):
@@ -70,6 +71,25 @@
 def padded(size, row_count):
     unit = SUB * row_count
     return -(-size // unit) * unit
+
+
+def strides_of(count, turned):
+    found = [1 << i for i in range(bits_of(count))]
+    return found[:1] + found[2:] + found[1:2] if turned else found
+
+
+def placed(value, strides):
+    found = 0
+    for stride in strides:
+        found = found * 2 + bit(value, stride)
+    return found
+
+
+def slot_of(place, strides):
+    found = 0
+    for i, stride in enumerate(reversed(strides)):
+        found += bit(place, 1 << i) * stride
+    return found
 
 
 class Chain:
@@ -122,7 +142,9 @@
     row_bits, col_bits, group_bits = bits_of(row_count), bits_of(col_count), bits_of(group)
     rows = row_count * SUB
     high, low = row // group, row % group
-    my_place = mirrored(low, group_bits)
+    lows = [strides_of(group, chunk in TURNED) for chunk in range(chunks)]
+    my_place = [placed(low, strides) for strides in lows]
+    highs = [group << i for i in range(col_bits)]
 
     barrier = pltpu.get_barrier_semaphore()
     for step in range(1, row_count):
@@ -183,9 +205,8 @@
         steps.append(ranked.pop(0))
         if ranked:
             steps.append(ranked.pop())
-    place = stage.at[
-        :, my_place, pl.ds(pl.multiple_of(mirrored(high, col_bits) * SUB, SUB), SUB)
-    ]
+    spot = pl.ds(pl.multiple_of(mirrored(high, col_bits) * SUB, SUB), SUB)
+    places = [stage.at[chunk, my_place[chunk], spot] for chunk in range(chunks)]
     sends = []
     for chunk in range(chunks):
         for step in steps:
@@ -194,7 +215,7 @@
                 vectors.at[
                     pl.ds(chunk * SUB, SUB), pl.ds(pl.multiple_of(other * length, 128), length)
                 ],
-                place.at[chunk], row_sems, chunk * row_count + step, {"row": other},
+                places[chunk], row_sems, chunk * row_count + step, {"row": other},
             )
             sends.append(item)
     own_rows = []
@@ -203,7 +224,7 @@
             vectors.at[
                 pl.ds(chunk * SUB, SUB), pl.ds(pl.multiple_of(row * length, 128), length)
             ],
-            place.at[chunk], local_sems.at[count + chunk],
+            places[chunk], local_sems.at[count + chunk],
         )
         item.start()
         own_rows.append(item)
@@ -285,12 +306,11 @@
 
         lax.fori_loop(0, last - first, body, 0)
 
-    def halving(source, target, sems, number):
+    def halving(source, target, sems, number, strides):
         total = source.shape[0]
         state = {"now": source}
         steps = []
-        for stage_number in range(row_bits):
-            stride = 1 << stage_number
+        for stage_number, stride in enumerate(strides):
             half = total >> (stage_number + 1)
             start = total - (total >> stage_number)
 
@@ -341,7 +361,7 @@
         base = chunk * col_count
 
         def begin():
-            place = wide.at[chunk, my_place, rows_of]
+            place = wide.at[chunk, my_place[chunk], rows_of]
             for step in range(col_count):
                 other = lax.rem(high + step, col_count)
                 item = remote(
@@ -358,7 +378,7 @@
 
             @pl.when(col == high)
             def _():
-                wide[chunk, my_place, rows_of, :] = solved[chunk]
+                wide[chunk, my_place[chunk], rows_of, :] = solved[chunk]
 
         def end():
             for step in range(1, col_count):
@@ -371,7 +391,7 @@
             for other in range(col_count):
                 item = remote(
                     solved.at[chunk],
-                    wide.at[chunk, my_place, pl.ds(other * SUB, SUB)],
+                    wide.at[chunk, my_place[chunk], pl.ds(other * SUB, SUB)],
                     cross_sems, base, {"row": row, "col": col}, base + other,
                 )
 
@@ -382,10 +402,10 @@
         return begin, end
 
     def spread(chunk):
-        strides = [group >> (i + 1) for i in range(group_bits)]
+        number = chunk * max(group_bits, 1)
         return Chain(
             [cross(chunk)]
-            + doubling(strides, wide.at[chunk], wide_sems, chunk * max(group_bits, 1), my_place, 1)
+            + doubling(lows[chunk][::-1], wide.at[chunk], wide_sems, number, my_place[chunk], 1)
         )
 
     far = {}
@@ -437,7 +457,7 @@
         lax.fori_loop(0, length // tile, body, 0)
         for place in range(group):
             for other in range(col_count):
-                slot = mirrored(place, group_bits) * col_count + other
+                slot = slot_of(place, lows[chunk]) * col_count + other
                 item = pltpu.make_async_copy(
                     here.at[chunk, place, pl.ds(other * SUB, SUB)],
                     out.at[pl.ds(slot * local + chunk * SUB, SUB)],
@@ -456,7 +476,7 @@
         columns = pl.ds(first * width, (last - first) * width)
         chain, state = halving(
             projection.at[chunk, :, columns], landing.at[chunk, :, columns], sum_sems,
-            sum_count[0] * row_bits,
+            sum_count[0] * row_bits, lows[chunk] + highs,
         )
         sum_count[0] += 1
         pieces[chunk].append((columns, state))
@@ -466,20 +486,21 @@
     def sum_gram(number):
         first, size = bounds[number]
         piece = size // row_count
-        place = mirrored(row, row_bits) * piece
+        strides = strides_of(row_count, number in GRAM_TURNED)
+        place = placed(row, strides) * piece
         target = gram.at[pl.ds(first, size)]
         base = gram_count[0] * 2 * row_bits
         gram_count[0] += 1
         chain, state = halving(
-            partial.at[pl.ds(first, size)], gram_landing.at[pl.ds(first, size)], gram_sems, base
+            partial.at[pl.ds(first, size)], gram_landing.at[pl.ds(first, size)], gram_sems, base,
+            strides,
         )
 
         def put():
             target[pl.ds(pl.multiple_of(place, SUB), piece), :] = state["now"][...]
 
-        strides = [1 << i for i in range(row_bits - 1, -1, -1)]
         later = doubling(
-            strides, target, gram_sems, base + row_bits, pl.multiple_of(place, SUB), piece
+            strides[::-1], target, gram_sems, base + row_bits, pl.multiple_of(place, SUB), piece
         )
         begin, end = later[0]
 
@@ -505,43 +526,41 @@
 
     per = len(steps)
     late = chunks - 1
-    due = [((number + 1) / len(sends), 2, number) for number in range(len(sends) - per)]
+    due = [((number + 1) / len(sends), 2, number) for number in range(len(sends))]
     due += [(0.04 + 0.124 * (i + 1) * 6 / count, 1, panel) for i, panel in enumerate(order)]
     groups = batches(count)
     closing = {panels[-1]: number for number, panels in enumerate(groups) if panels}
-    chains, taken, started = [], [], {}
+    chains, taken, started, here_now = [], [], {}, count
     for time, kind, number in sorted(due):
         for chain in chains:
             chain.tick_at(time)
         if kind == 2:
             arrive(number)
-            if (number + 1) % per == 0:
+            if (number + 1) % per == 0 and number < late * per:
                 chunk = number // per
                 take_rows(chunk)
                 taken.append(chunk)
                 started[chunk] = count
+                send_far(chunk)
+                if here_now < count:
+                    project(chunk, here_now, count)
         else:
             take_panel(number)
-            if number == 0:
-                for chunk in taken:
-                    send_far(chunk)
+            here_now = number
             inner(number)
-            if number in closing:
-                ready = [chunk for chunk in taken if started[chunk] > number]
-                for chunk in ready:
-                    project(chunk, number, started[chunk])
-                fresh = [sum_rows(chunk, number, started[chunk]) for chunk in ready]
-                for chunk in ready:
+            fresh = [sum_gram(closing[number])] if number in closing else []
+            for chunk in taken:
+                project(chunk, number, number + 1)
+                if number in closing:
+                    fresh.append(sum_rows(chunk, number, started[chunk]))
                     started[chunk] = number
-                fresh.append(sum_gram(closing[number]))
-                for chain in fresh:
-                    chain.tick_at(time)
-                chains += fresh
+            for chain in fresh:
+                chain.tick_at(time)
+            chains += fresh
     for chunk in range(late):
         if chunk not in far:
             send_far(chunk)
         if started[chunk] > 0:
-            project(chunk, 0, started[chunk])
             chain = sum_rows(chunk, 0, started[chunk])
             chain.tick()
             chains.append(chain)
@@ -564,35 +583,37 @@
             if chunk not in spreads and not busy(*row_chains[chunk]):
                 spreads[chunk] = gather(chunk)
                 spreads[chunk].tick()
-
-    for number in range(AFTER):
-        tick(*chains)
-    for number in range(late * per, len(sends)):
-        arrive(number)
     take_rows(late)
-    send_far(late)
     project(late, 0, count)
     final = sum_rows(late, 0, count)
     final.tick()
-    while busy(final):
-        tick(*chains, *spreads.values())
-        gather_ready()
-        build_ready()
-        final.tick()
-    final = gather(late)
-    final.tick()
+    updates = list(range(late))
+    finished = []
+
+    def compute():
+        if built[0]:
+            build_ready()
+        elif not finished:
+            finish()
+            finished.append(True)
+        elif updates and updates[0] in spreads and not busy(spreads[updates[0]]):
+            update(updates.pop(0))
+
+    for closing_step in range(2):
+        while busy(final):
+            final.tick()
+            if closing_step and late not in far:
+                send_far(late)
+            tick(*chains, *spreads.values())
+            gather_ready()
+            compute()
+        if closing_step == 0:
+            final = gather(late)
     while busy(*chains) or len(spreads) < late or busy(*spreads.values()):
         tick(*chains, *spreads.values())
         gather_ready()
-        build_ready()
-        final.tick()
-    build_ready()
-    finish()
-    for chunk in range(late):
-        update(chunk)
-        final.tick()
-    while busy(final):
-        final.tick()
+    while updates:
+        compute()
     update(late)
     for item in outs:
         item.wait()

time: 167 us -> 157 us (0.940)
  Pallas kernels: 161 us -> 152 us
    pallas_call x1, Pallas kernels: 161 us -> 152 us  [on_device(): pl.pallas_call(functools.partial(kernel, row_count, col_count), name='exc...]
where the time goes in v3:
time: 157 us; the launch traced here: 156 us
  Pallas kernels  152 us (97%)
  local copies, waits for them, and re-layouts  4.7 us (3%)
    pallas_call x1, Pallas kernels, on_device(): pl.pallas_call(functools.partial(kernel, row_count, col_count), name='exc...  152 us
    unnamed x1, local copies, waits for them, and re-layouts  4.7 us

profile of v3, /device:TPU:0, one launch (start us, length us, event | category | flops | bytes accessed | tf_op | source)
XLA Modules:
  0.0 156.4 jit_solution(10253606143066019272)
XLA Ops:
  0.0 151.7 %exchange.1 = f32[512,2048]{1,0:T(8,128)} custom-call(f32[32,32768]{1,0:T(8,128)} %vectors.1, f32[6,64,2048]{2,1,0:T(8,128)} %reflectors.1, f32[6,128,128]{2,1,0:T(8,128)} %factors.1), custom_call_target="tpu_custom_call" | custom-call | tf_op jit(solution)/shard_map/exchange/pallas_call | solution.py:642
  151.7 4.7 %copy.5 = f32[512,2048]{1,0:T(8,128)} copy(f32[512,2048]{1,0:T(8,128)} %exchange.1) | data formatting | bytes 8388608

commit v4 on v3

--- a/solution.py
+++ b/solution.py
@@ -10,7 +10,7 @@
 MESH = pl.DeviceIdType.MESH
 HIGHEST = lax.Precision.HIGHEST
 SUB = 8
-WIDER = -5
+WIDER = -3
 GAP0 = 0.025
 GAP = 0.12
 TURNED = (1,)
@@ -439,7 +439,7 @@
             pairs[pl.ds((2 * panel + 1) * width, width), :] = low_part
 
     outs = []
-    tile = 512 if length % 512 == 0 else length
+    tile = 1024 if length % 1024 == 0 else length
 
     def update(chunk):
         for item in far[chunk]:

time: 157 us -> 154 us (0.981)
  Pallas kernels: 152 us -> 149 us
    pallas_call x1, Pallas kernels: 152 us -> 149 us  [on_device(): pl.pallas_call(functools.partial(kernel, row_count, col_count), name='exc...]
where the time goes in v4:
time: 154 us
  Pallas kernels  149 us (97%)
  local copies, waits for them, and re-layouts  4.7 us (3%)
    pallas_call x1, Pallas kernels, on_device(): pl.pallas_call(functools.partial(kernel, row_count, col_count), name='exc...  149 us
    unnamed x1, local copies, waits for them, and re-layouts  4.7 us

profile of v4, /device:TPU:0, one launch (start us, length us, event | category | flops | bytes accessed | tf_op | source)
XLA Modules:
  0.0 153.9 jit_solution(15143631057736483569)
XLA Ops:
  0.0 149.2 %exchange.1 = f32[512,2048]{1,0:T(8,128)} custom-call(f32[32,32768]{1,0:T(8,128)} %vectors.1, f32[6,64,2048]{2,1,0:T(8,128)} %reflectors.1, f32[6,128,128]{2,1,0:T(8,128)} %factors.1), custom_call_target="tpu_custom_call" | custom-call | tf_op jit(solution)/shard_map/exchange/pallas_call | solution.py:642
  149.2 4.7 %copy.5 = f32[512,2048]{1,0:T(8,128)} copy(f32[512,2048]{1,0:T(8,128)} %exchange.1) | data formatting | bytes 8388608
